TPU v7x, 32 devices: a whole 2x2x4 slice. The times are simulated.
32 devices in a mesh: rep: 4 (over y, core), shard: 8 (over z, x).
Axes of the slice: x: 2, y: 2, z: 4, core: 2. Of those that a mesh axis runs over, the one named last changes fastest.
Arguments:
- hidden: bfloat16 [14336, 3584], P(('rep', 'shard')), may hold values from -144 to 144
- cotangent: bfloat16 [14336, 1024], P(('rep', 'shard')), may hold values from -6 to 6
- seq_ids: int32 [32, 448], P(('rep', 'shard')), may hold values from 0 to 3, as said below
- response_mask: int32 [32, 448], P(('rep', 'shard')), may hold values from 0 to 1, as said below
- group_ids: int32 [32, 4], P(('rep', 'shard')), may hold values from 0 to 15
- rewards: float32 [32, 4], P(('rep', 'shard')), may hold values from -6 to 6
- new_logp: float32 [32, 448], P(('rep', 'shard')), may hold values from -1.5 to -0.1
- old_logp: float32 [32, 448], P(('rep', 'shard')), may hold values from -1.5 to -0.1
- ref_logp: float32 [32, 448], P(('rep', 'shard')), may hold values from -1.5 to -0.1
- master: float32 [3, 3584, 1024], P(None, 'shard'), may hold values from -6 to 6
Outputs:
- new_master: float32 [3584, 1024], P('shard')
- rollout: bfloat16 [3, 3584, 2048], P(None, None, 'shard')
Inputs may be any that keep to these rules, and one draw needn't show every extreme that they name: `seq_ids`: each row numbers its device's 4 sequences in token order, never falling, each with one token or more. `response_mask`: within a sequence, prompt tokens come before response tokens; a sequence may have no response tokens.
All inputs are finite; a program needn't handle non-finite values.
Results may differ from a plain program's by a relative error of at most 0.0095.
Values may be sent and summed in bfloat16 or wider, within the bound.
A program may use at most 128 MiB of HBM per device.

v0:
```python
import jax
import jax.numpy as jnp
from jax import lax
from jax.sharding import PartitionSpec as P

HEAD = 128
KV_HEADS = 4
TP = 8
SEQ_DEV = 4


def token_coef(seq_row, mask_row, adv_row, new_row, old_row, ref_row):
    onehot = (seq_row[:, None] == jnp.arange(SEQ_DEV, dtype=jnp.int32)[None, :]).astype(jnp.float32)
    maskf = mask_row.astype(jnp.float32)
    lengths = jnp.maximum(jnp.dot(maskf, onehot, precision=lax.Precision.HIGHEST), 1.0)
    tok_len = jnp.dot(onehot, lengths, precision=lax.Precision.HIGHEST)
    tok_adv = jnp.dot(onehot, adv_row, precision=lax.Precision.HIGHEST)
    surrogate = -tok_adv * jnp.exp(new_row - old_row) + 0.2 * (1.0 - jnp.exp(ref_row - new_row))
    return maskf / tok_len * surrogate


def group_advantage(group_flat, reward_flat, stats):
    groups = stats.shape[1]
    onehot = (group_flat[:, None] == jnp.arange(groups, dtype=jnp.int32)[None, :]).astype(
        jnp.float32
    )
    count = jnp.maximum(stats[0], 1.0)
    mean = stats[1] / count
    spread = jnp.sqrt(jnp.maximum(stats[2] / count - mean * mean, 0.0))
    tok_mean = jnp.dot(onehot, mean, precision=lax.Precision.HIGHEST)
    tok_std = jnp.dot(onehot, jnp.maximum(spread, 0.5), precision=lax.Precision.HIGHEST)
    return (reward_flat - tok_mean) / tok_std


def group_sums(group_flat, reward_flat, groups):
    onehot = (group_flat[:, None] == jnp.arange(groups, dtype=jnp.int32)[None, :]).astype(
        jnp.float32
    )
    values = jnp.stack([jnp.ones_like(reward_flat), reward_flat, reward_flat * reward_flat], axis=0)
    return jnp.dot(values, onehot, precision=lax.Precision.HIGHEST)


def rounded(term):
    return lax.optimization_barrier(term.astype(jnp.bfloat16)).astype(jnp.float32)


def rollout_blocks(weights):
    layer_count = weights.shape[0]
    row_count = weights.shape[1]
    paired = weights.reshape(layer_count, row_count, 2, KV_HEADS, HEAD).transpose(0, 1, 3, 2, 4)
    paired = paired.reshape(layer_count, row_count, KV_HEADS, 2 * HEAD)
    by_rank = jnp.repeat(paired, TP // KV_HEADS, axis=2)
    copies = jnp.tile(by_rank, (1, 1, lax.axis_size("shard") // TP, 1))
    return copies.reshape(layer_count, row_count, lax.axis_size("shard") * 2 * HEAD)


def per_device(
    hidden,
    cotangent,
    seq_ids,
    response_mask,
    group_ids,
    rewards,
    new_logp,
    old_logp,
    ref_logp,
    master,
):
    n_rep = lax.axis_size("rep")
    n_shard = lax.axis_size("shard")
    groups = n_rep * n_shard * SEQ_DEV // 8
    rest_cols = lax.all_to_all(
        rollout_blocks(master[1:].astype(jnp.bfloat16)),
        "shard",
        split_axis=2,
        concat_axis=1,
        tiled=True,
    )
    local_sums = group_sums(group_ids[0], rewards[0], groups)
    stats = lax.psum(local_sums, ("rep", "shard"))
    advantage = group_advantage(group_ids[0], rewards[0], stats)
    coef = token_coef(
        seq_ids[0], response_mask[0], advantage, new_logp[0], old_logp[0], ref_logp[0]
    )
    delta = (coef[:, None] * cotangent.astype(jnp.float32)).astype(jnp.bfloat16)
    feature_count = hidden.shape[1]
    partial_value = lax.psum_scatter(
        rounded(
            lax.dot_general(
                hidden, delta, (((0,), (0,)), ((), ())), preferred_element_type=jnp.float32
            )
        ).astype(jnp.bfloat16),
        "shard",
        scatter_dimension=0,
        tiled=True,
    )
    grad = lax.psum(partial_value, "rep").astype(jnp.float32)
    squares = lax.psum(jnp.sum(grad * grad), "shard")
    rms = jnp.sqrt(squares / (feature_count * grad.shape[1]) + 1e-06)
    new_master = master[0] - 0.5 * grad / rms
    first_cols = lax.all_to_all(
        rollout_blocks(new_master[None].astype(jnp.bfloat16)),
        "shard",
        split_axis=2,
        concat_axis=1,
        tiled=True,
    )
    rollout = jnp.concatenate([first_cols, rest_cols], axis=0)
    return (new_master, rollout)


def solution(mesh):
    in_specs = (
        P(("rep", "shard"), None),
        P(("rep", "shard"), None),
        P(("rep", "shard"), None),
        P(("rep", "shard"), None),
        P(("rep", "shard"), None),
        P(("rep", "shard"), None),
        P(("rep", "shard"), None),
        P(("rep", "shard"), None),
        P(("rep", "shard"), None),
        P(None, "shard", None),
    )
    out_specs = (P("shard", None), P(None, None, "shard"))
    return jax.shard_map(
        per_device, mesh=mesh, in_specs=in_specs, out_specs=out_specs, check_vma=False
    )
```

profile of v0, /device:TPU:0, one launch (start us, length us, event | category | flops | bytes accessed | tf_op | source)
XLA Modules:
  0.0 468.4 jit_solution(8274017862780211825)
XLA Ops:
  9.0 41.9 %psum.21 = f32[3,16]{1,0:T(4,128)S(1)} all-reduce(f32[3,16]{1,0:T(4,128)S(1)} %fusion.15), channel_id=1, replica_groups=mesh['rep'=4,'shard'=8] {'rep','shard'}, use_global_device_ids=true, to_apply=%region_0.0 | all-reduce | flops 48 | bytes 384 | tf_op jit(solution)/shard_map/psum | solution.py:80
  55.3 1.0 fusion.11
  57.1 7.5 %fusion = bf16[3584,1024]{0,1:T(8,128)(2,1)} fusion(bf16[448,3584]{1,0:T(8,128)(2,1)S(1)} %copy-done, bf16[448,1024]{1,0:T(8,128)(2,1)} %param.11, f32[448]{0:T(512)S(1)} %add_multiply_fusion), kind=kOutput, calls=%fused_computation.1 | convolution fusion | flops 3293380608 | bytes 11470592 | tf_op jit(solution)/shard_map/dot_general | solution.py:89
  64.6 10.4 %copy.47 = bf16[3584,1024]{1,0:T(8,128)(2,1)} copy(bf16[3584,1024]{0,1:T(8,128)(2,1)} %fusion) | data formatting | bytes 14680064
  75.0 2.3 slice.36
  77.4 2.3 reshape.41
  79.6 5.7 %copy.49 = bf16[2,448,2,4,128]{1,0,4,2,3:T(2,128)(2,1)S(1)} copy(bf16[2,448,2,4,128]{4,3,2,1,0:T(4,128)(2,1)} %reshape.41) | data formatting | bytes 3670016 | tf_op jit(solution)/shard_map/transpose | solution.py:50
  85.3 4.2 broadcast_in_dim.15
  89.5 5.3 %all-to-all-start.1 = ((bf16[2,448,2048]{1,0,2:T(2,128)(2,1)}), bf16[2,448,2048]{1,0,2:T(2,128)(2,1)}, u32[]{:S(2)}, u32[]{:S(2)}) async-start(bf16[2,448,2048]{1,0,2:T(2,128)(2,1)} %bitcast.83), calls=%async_computation.1 | async-start | bytes 8388608 | tf_op jit(solution)/shard_map/all_to_all | solution.py:72
  94.9 188.3 %reduce-scatter.4.cloned.1.call-done = bf16[448,1024]{1,0:T(8,128)(2,1)} async-done(((bf16[3584,1024]{1,0:T(8,128)(2,1)}), bf16[448,1024]{1,0:T(8,128)(2,1)}) %reduce-scatter.4.cloned.1.call-update) | async-done | bytes 917520
  283.2 2.2 copy.48
  285.4 36.1 %all-reduce.2.cloned.1.call-done = bf16[448,1024]{0,1:T(8,128)(2,1)} async-done(((bf16[448,1024]{0,1:T(8,128)(2,1)}), bf16[448,1024]{0,1:T(8,128)(2,1)}) %all-reduce.2.cloned.1.call-update) | async-done | bytes 917520 | tf_op jit(solution)/shard_map/psum | solution.py:97
  321.5 2.4 fusion.3
  323.9 1.9 copy.51
  325.7 22.1 %psum.23 = f32[]{:T(128)} all-reduce(f32[]{:T(128)} %fusion.3), channel_id=1, replica_groups=mesh['rep'=4,'shard'=8] {'shard'}, use_global_device_ids=true, to_apply=%region_4.0 | all-reduce | flops 1 | bytes 8 | tf_op jit(solution)/shard_map/psum | solution.py:98
  348.6 3.0 fusion.36
  351.6 3.6 copy.33
  355.2 2.7 reshape.40
  358.6 2.5 broadcast_in_dim.6
  361.1 5.3 %broadcast_in_dim.14 = bf16[1,448,2048]{2,1,0:T(8,128)(2,1)} reshape(bf16[448,4,2,256]{3,2,1,0:T(2,128)(2,1)} %broadcast_in_dim.6) | data formatting | bytes 3670016 | tf_op jit(solution)/shard_map/broadcast_in_dim | solution.py:52
  366.4 10.7 %copy.35 = bf16[1,448,2048]{1,0,2:T(2,128)(2,1)} copy(bf16[1,448,2048]{2,1,0:T(8,128)(2,1)} %broadcast_in_dim.14) | data formatting | bytes 3670016 | tf_op jit(solution)/shard_map/broadcast_in_dim | solution.py:52
  377.6 15.4 %reduce = bf16[2048,448]{1,0:T(8,128)(2,1)} reduce(bf16[2048,1,448]{2,1,0:T(2,128)(2,1)} %bitcast.84, bf16[]{:T(256)} %broadcast.50), dimensions={1}, to_apply=%bitcast.77.reduce_sub_computation | reduce | bytes 3670018
  393.1 6.8 %reshape.57 = bf16[8,2,57344]{2,1,0:T(2,128)(2,1)} reshape(bf16[2048,448]{1,0:T(8,128)(2,1)} %reduce) | data formatting | bytes 3670016
  399.8 4.3 all-to-all-start
  404.2 11.1 %copy.46 = bf16[2,448,8,256]{3,1,2,0:T(8,128)(2,1)} copy(bf16[2,448,8,256]{1,0,3,2:T(2,128)(2,1)} %bitcast.27) | data formatting | bytes 7340032 | tf_op jit(solution)/shard_map/all_to_all | solution.py:72
  415.3 1.7 copy.42
  417.0 25.9 %all-to-all-done = bf16[8,2,57344]{2,1,0:T(2,128)(2,1)} async-done(((bf16[8,2,57344]{2,1,0:T(2,128)(2,1)}), bf16[8,2,57344]{2,1,0:T(2,128)(2,1)}, u32[]{:S(2)}, u32[]{:S(2)}) %all-to-all-start) | async-done | bytes 1835040 | tf_op jit(solution)/shard_map/all_to_all | solution.py:101
  442.9 7.2 %reshape.58 = bf16[2048,1,448]{2,1,0:T(2,128)(2,1)} reshape(bf16[8,2,57344]{2,1,0:T(2,128)(2,1)} %all-to-all-done) | data formatting | bytes 3670016
  450.1 2.8 copy.50
  452.9 3.0 copy.43
  455.8 2.0 copy.37
  458.4 2.9 pad_maximum_fusion
  (28 shorter events, 9.0 us)
Async XLA Ops:
  7.2 49.9 %copy-start = (bf16[448,3584]{1,0:T(8,128)(2,1)S(1)}, bf16[448,3584]{1,0:T(8,128)(2,1)}, u32[]{:S(2)}) copy-start(bf16[448,3584]{1,0:T(8,128)(2,1)} %param.10) | copy-start | bytes 9633796
  7.2 276.0 %reduce-scatter.4.cloned.1.call-start = ((), (), s32[]{:S(2)}) async-start(), calls=%async_computation.4 | async-start | bytes 8257536
  89.5 310.4 %all-to-all-start.1 = ((bf16[2,448,2048]{1,0,2:T(2,128)(2,1)}), bf16[2,448,2048]{1,0,2:T(2,128)(2,1)}, u32[]{:S(2)}, u32[]{:S(2)}) async-start(bf16[2,448,2048]{1,0,2:T(2,128)(2,1)} %bitcast.83), calls=%async_computation.1 | async-start | bytes 8388608 | tf_op jit(solution)/shard_map/all_to_all | solution.py:72
  94.8 226.7 %all-reduce.2.cloned.1.call-start = ((), (), s32[]{:S(2)}) async-start(), calls=%async_computation.3 | async-start | bytes 2097152 | tf_op jit(solution)/shard_map/psum | solution.py:97
  285.4 38.5 %slice-start = ((f32[3,448,1024]{2,1,0:T(8,128)}), f32[1,448,1024]{2,1,0:T(8,128)S(1)}, s32[]{:S(2)}) async-start(f32[3,448,1024]{2,1,0:T(8,128)} %param.19), calls=%async_computation.5 | async-start | bytes 3670016 | tf_op jit(solution)/shard_map/slice | solution.py:100
  323.9 24.7 %copy-start.3 = (bf16[448,1024]{0,1:T(8,128)(2,1)S(1)}, bf16[448,1024]{0,1:T(8,128)(2,1)}, u32[]{:S(2)}) copy-start(bf16[448,1024]{0,1:T(8,128)(2,1)} %all-reduce.2.cloned.1.call-done) | copy-start | bytes 2752516
  399.8 43.1 %all-to-all-start = ((bf16[8,2,57344]{2,1,0:T(2,128)(2,1)}), bf16[8,2,57344]{2,1,0:T(2,128)(2,1)}, u32[]{:S(2)}, u32[]{:S(2)}) async-start(bf16[8,2,57344]{2,1,0:T(2,128)(2,1)} %reshape.57), calls=%async_computation | async-start | bytes 3670016 | tf_op jit(solution)/shard_map/all_to_all | solution.py:101
  455.8 2.6 copy-start.2
  458.4 3.1 copy-start.1
Sparse Core Ops, SparseCore 0:
  75.2 207.9 reduce-scatter.3
  286.1 35.3 all-reduce.1
where the time goes:
time: 470 us; the launch traced here: 468 us
  waiting for transfers between devices  250 us (53%)
  local copies, waits for them, and re-layouts  90.3 us (19%)
  blocking collectives  64.1 us (14%)
  other arithmetic  26 us (6%)
  between operations  14.8 us (3%)
  matrix products  13.1 us (3%)
  starting transfers between devices  9.74 us (2%)
    unnamed x3, waiting for transfers between devices  188 us
    psum x1, blocking collectives, per_device(): stats = lax.psum(local_sums, ('rep', 'shard'))  41.9 us
    psum x1, waiting for transfers between devices, per_device(): grad = lax.psum(partial_value, 'rep').astype(jnp.float32)  36.1 us
    unnamed x16, local copies, waits for them, and re-layouts  34.2 us
    all_to_all x1, waiting for transfers between devices, per_device(): lax.all_to_all(rollout_blocks(new_master[None].astype(jnp.bfloat16)), 'sh...  25.9 us
    broadcast_in_dim x4, local copies, waits for them, and re-layouts, rollout_blocks(): by_rank = jnp.repeat(paired, TP // KV_HEADS, axis=2)  22.7 us
    psum x1, blocking collectives, per_device(): squares = lax.psum(jnp.sum(grad * grad), 'shard')  22.1 us
    unnamed x1, other arithmetic  15.4 us
  transfers between devices with their start and end apart: 4, of which 3 were waited for; matrix products, arithmetic and copies ran while one was open for 18% of the time, Pallas kernels for 0%

commit v1 on v0

--- a/solution.py
+++ b/solution.py
@@ -77,7 +77,7 @@
         tiled=True,
     )
     local_sums = group_sums(group_ids[0], rewards[0], groups)
-    stats = lax.psum(local_sums, ("rep", "shard"))
+    stats = jnp.sum(lax.all_gather(local_sums, ("rep", "shard")), axis=0)
     advantage = group_advantage(group_ids[0], rewards[0], stats)
     coef = token_coef(
         seq_ids[0], response_mask[0], advantage, new_logp[0], old_logp[0], ref_logp[0]

time: 470 us -> 495 us (1.053)
  blocking collectives: 64.1 us -> 92.2 us
    all_gather x0 -> x1, blocking collectives: none -> 70 us  [per_device(): stats = jnp.sum(lax.all_gather(local_sums, ('rep', 'shard')), axis=0)]
    psum x1 -> x0, blocking collectives: 41.9 us -> none  [per_device(): stats = lax.psum(local_sums, ('rep', 'shard'))]
  transfers between devices with their start and end apart: 4 -> 4, of which waited for: 3 -> 3; matrix products, arithmetic and copies ran while one was open for 18% -> 17% of each run, Pallas kernels for 0% -> 0%
where the time goes in v1:
time: 495 us; the launch traced here: 493 us
  waiting for transfers between devices  248 us (50%)
  blocking collectives  92.2 us (19%)
  local copies, waits for them, and re-layouts  90.2 us (18%)
  other arithmetic  26.1 us (5%)
  between operations  14.8 us (3%)
  matrix products  13.1 us (3%)
  starting transfers between devices  8.93 us (2%)
    unnamed x3, waiting for transfers between devices  186 us
    all_gather x1, blocking collectives, per_device(): stats = jnp.sum(lax.all_gather(local_sums, ('rep', 'shard')), axis=0)  70 us
    psum x1, waiting for transfers between devices, per_device(): grad = lax.psum(partial_value, 'rep').astype(jnp.float32)  36.1 us
    unnamed x16, local copies, waits for them, and re-layouts  34.2 us
    all_to_all x1, waiting for transfers between devices, per_device(): lax.all_to_all(rollout_blocks(new_master[None].astype(jnp.bfloat16)), 'sh...  25.9 us
    broadcast_in_dim x4, local copies, waits for them, and re-layouts, rollout_blocks(): by_rank = jnp.repeat(paired, TP // KV_HEADS, axis=2)  22.7 us
    psum x1, blocking collectives, per_device(): squares = lax.psum(jnp.sum(grad * grad), 'shard')  22.1 us
    unnamed x1, other arithmetic  15.4 us
  transfers between devices with their start and end apart: 4, of which 3 were waited for; matrix products, arithmetic and copies ran while one was open for 17% of the time, Pallas kernels for 0%

profile of v1, /device:TPU:0, one launch (start us, length us, event | category | flops | bytes accessed | tf_op | source)
XLA Modules:
  0.0 493.0 jit_solution(1659820713276005590)
XLA Ops:
  9.0 70.0 %all-gather.1 = f32[32,3,16]{2,1,0:T(4,128)S(1)} all-gather(f32[1,3,16]{2,1,0:T(4,128)S(1)} %convolution_bitcast_fusion), channel_id=2, replica_groups=mesh['rep'=4,'shard'=8] {'rep','shard'}, dimensions={0}, use_global_device_ids=true | all-gather | bytes 6336 | tf_op jit(solution)/shard_map/all_gather | solution.py:80
  83.4 1.0 fusion.11
  85.2 7.5 %fusion = bf16[3584,1024]{0,1:T(8,128)(2,1)} fusion(bf16[448,3584]{1,0:T(8,128)(2,1)S(1)} %copy-done, bf16[448,1024]{1,0:T(8,128)(2,1)} %param.11, f32[448]{0:T(512)S(1)} %add_multiply_fusion), kind=kOutput, calls=%fused_computation.1 | convolution fusion | flops 3293380608 | bytes 11470592 | tf_op jit(solution)/shard_map/dot_general | solution.py:89
  92.7 10.4 %copy.47 = bf16[3584,1024]{1,0:T(8,128)(2,1)} copy(bf16[3584,1024]{0,1:T(8,128)(2,1)} %fusion) | data formatting | bytes 14680064
  103.2 2.3 slice.36
  105.5 2.3 reshape.41
  107.8 5.6 %copy.49 = bf16[2,448,2,4,128]{1,0,4,2,3:T(2,128)(2,1)S(1)} copy(bf16[2,448,2,4,128]{4,3,2,1,0:T(4,128)(2,1)} %reshape.41) | data formatting | bytes 3670016 | tf_op jit(solution)/shard_map/transpose | solution.py:50
  113.4 4.2 broadcast_in_dim.15
  117.6 4.5 all-to-all-start.1
  122.2 185.6 %reduce-scatter.4.cloned.1.call-done = bf16[448,1024]{1,0:T(8,128)(2,1)} async-done(((bf16[3584,1024]{1,0:T(8,128)(2,1)}), bf16[448,1024]{1,0:T(8,128)(2,1)}) %reduce-scatter.4.cloned.1.call-update) | async-done | bytes 917520
  307.8 2.2 copy.48
  310.1 36.1 %all-reduce.2.cloned.1.call-done = bf16[448,1024]{0,1:T(8,128)(2,1)} async-done(((bf16[448,1024]{0,1:T(8,128)(2,1)}), bf16[448,1024]{0,1:T(8,128)(2,1)}) %all-reduce.2.cloned.1.call-update) | async-done | bytes 917520 | tf_op jit(solution)/shard_map/psum | solution.py:97
  346.1 2.4 fusion.3
  348.5 1.9 copy.51
  350.4 22.1 %psum.15 = f32[]{:T(128)} all-reduce(f32[]{:T(128)} %fusion.3), channel_id=1, replica_groups=mesh['rep'=4,'shard'=8] {'shard'}, use_global_device_ids=true, to_apply=%region_4.0 | all-reduce | flops 1 | bytes 8 | tf_op jit(solution)/shard_map/psum | solution.py:98
  373.2 3.0 fusion.35
  376.2 3.6 copy.33
  379.9 2.7 reshape.40
  383.2 2.5 broadcast_in_dim.6
  385.7 5.3 %broadcast_in_dim.14 = bf16[1,448,2048]{2,1,0:T(8,128)(2,1)} reshape(bf16[448,4,2,256]{3,2,1,0:T(2,128)(2,1)} %broadcast_in_dim.6) | data formatting | bytes 3670016 | tf_op jit(solution)/shard_map/broadcast_in_dim | solution.py:52
  391.0 10.7 %copy.35 = bf16[1,448,2048]{1,0,2:T(2,128)(2,1)} copy(bf16[1,448,2048]{2,1,0:T(8,128)(2,1)} %broadcast_in_dim.14) | data formatting | bytes 3670016 | tf_op jit(solution)/shard_map/broadcast_in_dim | solution.py:52
  402.3 15.4 %reduce.1 = bf16[2048,448]{1,0:T(8,128)(2,1)} reduce(bf16[2048,1,448]{2,1,0:T(2,128)(2,1)} %bitcast.86, bf16[]{:T(256)} %broadcast.50), dimensions={1}, to_apply=%bitcast.79.reduce_sub_computation | reduce | bytes 3670018
  417.7 6.8 %reshape.61 = bf16[8,2,57344]{2,1,0:T(2,128)(2,1)} reshape(bf16[2048,448]{1,0:T(8,128)(2,1)} %reduce.1) | data formatting | bytes 3670016
  424.5 4.3 all-to-all-start
  428.8 11.1 %copy.46 = bf16[2,448,8,256]{3,1,2,0:T(8,128)(2,1)} copy(bf16[2,448,8,256]{1,0,3,2:T(2,128)(2,1)} %bitcast.28) | data formatting | bytes 7340032 | tf_op jit(solution)/shard_map/all_to_all | solution.py:72
  439.9 1.7 copy.42
  441.7 25.9 %all-to-all-done = bf16[8,2,57344]{2,1,0:T(2,128)(2,1)} async-done(((bf16[8,2,57344]{2,1,0:T(2,128)(2,1)}), bf16[8,2,57344]{2,1,0:T(2,128)(2,1)}, u32[]{:S(2)}, u32[]{:S(2)}) %all-to-all-start) | async-done | bytes 1835040 | tf_op jit(solution)/shard_map/all_to_all | solution.py:101
  467.5 7.2 %reshape.62 = bf16[2048,1,448]{2,1,0:T(2,128)(2,1)} reshape(bf16[8,2,57344]{2,1,0:T(2,128)(2,1)} %all-to-all-done) | data formatting | bytes 3670016
  474.7 2.8 copy.50
  477.5 3.0 copy.43
  480.5 2.0 copy.37
  483.1 2.9 pad_maximum_fusion
  (29 shorter events, 9.1 us)
Async XLA Ops:
  7.2 78.1 %copy-start = (bf16[448,3584]{1,0:T(8,128)(2,1)S(1)}, bf16[448,3584]{1,0:T(8,128)(2,1)}, u32[]{:S(2)}) copy-start(bf16[448,3584]{1,0:T(8,128)(2,1)} %param.10) | copy-start | bytes 9633796
  7.2 300.6 %reduce-scatter.4.cloned.1.call-start = ((), (), s32[]{:S(2)}) async-start(), calls=%async_computation.4 | async-start | bytes 8257536
  117.6 306.9 %all-to-all-start.1 = ((bf16[2,448,2048]{1,0,2:T(2,128)(2,1)}), bf16[2,448,2048]{1,0,2:T(2,128)(2,1)}, u32[]{:S(2)}, u32[]{:S(2)}) async-start(bf16[2,448,2048]{1,0,2:T(2,128)(2,1)} %bitcast.85), calls=%async_computation.1 | async-start | bytes 8388608 | tf_op jit(solution)/shard_map/all_to_all | solution.py:72
  122.1 224.0 %all-reduce.2.cloned.1.call-start = ((), (), s32[]{:S(2)}) async-start(), calls=%async_computation.3 | async-start | bytes 2097152 | tf_op jit(solution)/shard_map/psum | solution.py:97
  310.0 38.5 %slice-start = ((f32[3,448,1024]{2,1,0:T(8,128)}), f32[1,448,1024]{2,1,0:T(8,128)S(1)}, s32[]{:S(2)}) async-start(f32[3,448,1024]{2,1,0:T(8,128)} %param.19), calls=%async_computation.5 | async-start | bytes 3670016 | tf_op jit(solution)/shard_map/slice | solution.py:100
  348.5 24.7 %copy-start.3 = (bf16[448,1024]{0,1:T(8,128)(2,1)S(1)}, bf16[448,1024]{0,1:T(8,128)(2,1)}, u32[]{:S(2)}) copy-start(bf16[448,1024]{0,1:T(8,128)(2,1)} %all-reduce.2.cloned.1.call-done) | copy-start | bytes 2752516
  424.5 43.1 %all-to-all-start = ((bf16[8,2,57344]{2,1,0:T(2,128)(2,1)}), bf16[8,2,57344]{2,1,0:T(2,128)(2,1)}, u32[]{:S(2)}, u32[]{:S(2)}) async-start(bf16[8,2,57344]{2,1,0:T(2,128)(2,1)} %reshape.61), calls=%async_computation | async-start | bytes 3670016 | tf_op jit(solution)/shard_map/all_to_all | solution.py:101
  480.5 2.6 copy-start.2
  483.1 3.1 copy-start.1
Sparse Core Ops, SparseCore 0:
  103.3 204.4 reduce-scatter.3
  310.7 35.3 all-reduce.1
